TPU v7x, 32 devices: a whole 2x2x4 slice. The times are simulated.
32 devices in a mesh: grp: 2 (over y), tile: 4 (over z), coil: 2 (over x), spk: 2 (over core).
Axes of the slice: x: 2, y: 2, z: 4, core: 2. Of those that a mesh axis runs over, the one named last changes fastest.
Arguments:
- coil_maps: float32 [2, 512, 2, 256], P('coil', ('grp', 'tile', 'spk')), parts along dimension 1, may hold values from -6 to 6
- kspace_data: bfloat16 [2, 128, 2, 256], P('coil', ('grp', 'tile', 'spk')), parts along dimension 1, may hold values from -24 to 24
- interp_weights: bfloat16 [128, 6, 256], P(('grp', 'tile', 'spk')), parts along dimension 0, may hold values from 0.099609375 to 1
- sample_bins: int32 [128, 256], P(('grp', 'tile', 'spk')), parts along dimension 0, may hold values from 0 to 65535, as said below
- spoke_count: int32 [16], P(('grp', 'tile', 'spk')), parts along dimension 0, may hold values from 1 to 8, 32 in all
- thresholds: float32 [3], replicated, may hold values from 0.05 to 0.3
Outputs:
- image: float32 [512, 2, 256], P(('grp', 'tile', 'spk')), parts along dimension 0
There are 2 independent parts, one for each index of `grp`. A program takes and returns all parts, laid end to end along the dimension named above; an argument that names none is the same for every part. Nothing has to cross between parts.
Inputs may be any that keep to these rules, and one draw needn't show every extreme that they name: `sample_bins`: sample k of each spoke lies on a straight line through cell (128, 128), at offset k - 128 along the spoke's direction, coordinates taken modulo 256. `spoke_count`: each independent slice has its own 8 counts, and the whole array holds one such block of counts per slice. The 8 counts of each slice sum to 32. In every draw, at least one device of each slice holds 8 live spokes. A device's live spokes are its first ones.
All inputs are finite; a program needn't handle non-finite values.
Results may differ from a plain program's by a relative error of at most 0.0016.
Values may be sent and summed in bfloat16 or wider, within the bound.
A program may use at most 64 MiB of HBM per device.

v0:
```python
import math
import jax
import jax.numpy as jnp
from jax import lax
from jax.sharding import PartitionSpec as P

N = 256
RO = 256
SPK_DEV = 8
LEVELS = 3
ITERS = 4
HIGH = lax.Precision.HIGHEST
STEP_SIZE = 0.5
RSQRT2 = 0.7071067811865476


def dft_table(length, direction):
    positions = jnp.arange(length, dtype=jnp.int32)
    phases = positions[:, None] * positions[None, :] % length
    angles = phases.astype(jnp.float32) * jnp.float32(2.0 * math.pi / length)
    norm_scale = 1.0 / math.sqrt(length)
    cosine = jnp.cos(angles) * norm_scale
    sine_tab = jnp.sin(angles) * norm_scale
    top_rows = jnp.stack([cosine, -direction * sine_tab], axis=1)
    bottom = jnp.stack([direction * sine_tab, cosine], axis=1)
    return jnp.stack([top_rows, bottom], axis=0)


def haar_matrix(length, levels):
    haar_mat = jnp.eye(length, dtype=jnp.float32)
    positions = jnp.arange(length, dtype=jnp.int32)
    out_i = positions[:, None]
    in_j = positions[None, :]
    for level_num in range(levels):
        span_len = length >> level_num
        half_len = span_len // 2
        low_hit = (out_i < half_len) & ((in_j == 2 * out_i) | (in_j == 2 * out_i + 1))
        high_pos = out_i - half_len
        high_hit = (
            (out_i >= half_len)
            & (out_i < span_len)
            & ((in_j == 2 * high_pos) | (in_j == 2 * high_pos + 1))
        )
        sign_val = jnp.where(in_j == 2 * high_pos + 1, -1.0, 1.0)
        step_mat = jnp.where(low_hit, RSQRT2, jnp.where(high_hit, sign_val * RSQRT2, 0.0))
        step_mat = step_mat + jnp.where((out_i >= span_len) & (in_j == out_i), 1.0, 0.0)
        haar_mat = jnp.dot(step_mat.astype(jnp.float32), haar_mat, precision=HIGH)
    return haar_mat


def haar_labels(length, levels):
    positions = jnp.arange(length, dtype=jnp.int32)
    band_label = jnp.ones((length,), jnp.int32)
    for level_num in range(1, levels + 1):
        band_label = band_label + (positions < length >> level_num).astype(jnp.int32)
    return band_label


def wavelet_shrink(target, thresholds, levels):
    row_count, pair_dim, col_count = target.shape
    block_len = 2**levels
    row_haar = haar_matrix(block_len, levels)
    col_haar = haar_matrix(col_count, levels)
    grouped = target.reshape(row_count // block_len, block_len, pair_dim, col_count)
    coeffs = jnp.einsum("ij,gjpc->gipc", row_haar, grouped, precision=HIGH)
    coeffs = jnp.einsum("gipc,kc->gipk", coeffs, col_haar, precision=HIGH)
    band_min = jnp.minimum(
        haar_labels(block_len, levels)[:, None], haar_labels(col_count, levels)[None, :]
    )
    active = band_min <= levels
    limits = jnp.ones(band_min.shape, jnp.float32)
    for level_num in range(levels):
        limits = jnp.where(band_min == level_num + 1, thresholds[level_num], limits)
    magnitude = jnp.sqrt(coeffs[:, :, 0] ** 2 + coeffs[:, :, 1] ** 2)
    factor = jnp.maximum(magnitude - limits, 0.0) / jnp.maximum(magnitude, limits)
    factor = jnp.where(active, factor, 1.0)
    shrunk = coeffs * factor[:, :, None, :]
    restored = jnp.einsum("gipk,kc->gipc", shrunk, col_haar, precision=HIGH)
    restored = jnp.einsum("ij,gipc->gjpc", row_haar, restored, precision=HIGH)
    return restored.reshape(row_count, pair_dim, col_count)


def complex_mul(left, right):
    real_part = left[:, 0] * right[:, 0] - left[:, 1] * right[:, 1]
    imag_part = left[:, 0] * right[:, 1] + left[:, 1] * right[:, 0]
    return jnp.stack([real_part, imag_part], axis=1)


def conj_mul(left, right):
    real_part = left[:, 0] * right[:, 0] + left[:, 1] * right[:, 1]
    imag_part = left[:, 0] * right[:, 1] - left[:, 1] * right[:, 0]
    return jnp.stack([real_part, imag_part], axis=1)


def interp_tables(load_bins, load_interp):
    grid_ids = jnp.arange(N, dtype=jnp.int32)
    row_bins = load_bins // N
    col_bins = load_bins % N
    zero_val = jnp.zeros((), jnp.bfloat16)
    row_table = jnp.zeros((load_bins.shape[0], load_bins.shape[1], N), jnp.bfloat16)
    col_table = jnp.zeros((load_bins.shape[0], N, load_bins.shape[1]), jnp.bfloat16)
    for tap_index in range(3):
        row_hit = grid_ids[None, None, :] == ((row_bins + tap_index - 1) % N)[:, :, None]
        row_table = row_table + jnp.where(
            row_hit, load_interp[:, tap_index, :][:, :, None], zero_val
        )
        col_hit = grid_ids[None, :, None] == ((col_bins + tap_index - 1) % N)[:, None, :]
        col_table = col_table + jnp.where(
            col_hit, load_interp[:, 3 + tap_index, :][:, None, :], zero_val
        )
    return (row_table, col_table)


def local(coil_maps, kspace_data, interp_weights, sample_bins, spoke_count, thresholds):
    blocks = lax.axis_size(("tile", "spk"))
    row_count = coil_maps.shape[1]
    live_total = blocks * SPK_DEV // 2
    coil_sens = coil_maps[0]
    measured = kspace_data[0]
    my_index = lax.axis_index(("tile", "spk"))
    counts = lax.all_gather(spoke_count, ("tile", "spk"), axis=0, tiled=True)
    prefix = jnp.cumsum(counts) - counts
    per_peer = -(-SPK_DEV // blocks)
    peer_ids = jnp.arange(blocks, dtype=jnp.int32)
    first_slot = (peer_ids - prefix[my_index]) % blocks
    slot_index = first_slot[:, None] + blocks * jnp.arange(per_peer, dtype=jnp.int32)[None, :]
    picked = jnp.clip(slot_index, 0, SPK_DEV - 1)
    values = jnp.concatenate([measured, interp_weights], axis=1)
    got_values = lax.all_to_all(
        values[picked], ("tile", "spk"), split_axis=0, concat_axis=0, tiled=True
    )
    got_bins = lax.all_to_all(
        sample_bins[picked], ("tile", "spk"), split_axis=0, concat_axis=0, tiled=True
    )
    my_share = SPK_DEV // 2
    wanted = my_index + blocks * jnp.arange(my_share, dtype=jnp.int32)
    source = jnp.sum((prefix[None, :] <= wanted[:, None]).astype(jnp.int32), axis=1) - 1
    depth_at = (wanted - prefix[source]) // blocks
    loaded = got_values[source, depth_at]
    load_bins = got_bins[source, depth_at]
    load_data = loaded[:, 0:2]
    load_interp = loaded[:, 2:8]
    row_table, col_table = interp_tables(load_bins, load_interp)
    n_load = row_table.shape[0]
    offset = jnp.abs(jnp.arange(RO, dtype=jnp.int32) - RO // 2).astype(jnp.float32)
    density = (offset + 0.5) * (N / (3.0 * RO * live_total))
    target_data = load_data.astype(jnp.float32)
    fwd_table = dft_table(N, 1.0)
    inv_table = dft_table(N, -1.0)

    def grid_rows(weighted):

        def grid_term(row_start, piece_rows):

            def grid_one_spoke(spoke_index, partial_value):
                row_one = lax.dynamic_index_in_dim(row_table, spoke_index, 0, keepdims=False)
                col_one = lax.dynamic_index_in_dim(col_table, spoke_index, 0, keepdims=False)
                col_slice = col_one.astype(jnp.float32)
                residue = lax.dynamic_index_in_dim(weighted, spoke_index, 0, keepdims=False)
                smeared = (col_slice[:, None, :] * residue[None, :, :]).astype(jnp.bfloat16)
                added = jnp.dot(
                    smeared.reshape(piece_rows * 2, RO), row_one, preferred_element_type=jnp.float32
                )
                return partial_value + added.reshape(piece_rows, 2, N)

            return lax.fori_loop(
                0, my_share, grid_one_spoke, jnp.zeros((piece_rows, 2, N), jnp.float32)
            )

        return grid_term

    estimate = jnp.zeros((row_count, 2, N), jnp.float32)
    for iteration in range(ITERS):
        if iteration == 0:
            weighted = -density[None, None, :] * target_data
        else:
            coil_image = complex_mul(coil_sens, estimate)
            half_done = jnp.einsum("rpc,pcqv->rqv", coil_image, fwd_table, precision=HIGH)
            turned = lax.all_to_all(
                half_done, ("tile", "spk"), split_axis=2, concat_axis=0, tiled=True
            )
            kspace = jnp.einsum("rpv,prqu->vqu", turned, fwd_table, precision=HIGH).astype(
                jnp.bfloat16
            )
            piece = lax.all_gather(kspace, ("tile", "spk"), axis=0, tiled=True)
            fold_piece_rows = piece.shape[0]
            flat_piece = piece.reshape(fold_piece_rows * 2, N)

            def fold_one_spoke(spoke_index, partial_value):
                row_one = lax.dynamic_index_in_dim(row_table, spoke_index, 0, keepdims=False)
                col_one = lax.dynamic_index_in_dim(col_table, spoke_index, 0, keepdims=False)
                inner_sum = lax.dot_general(
                    flat_piece,
                    row_one,
                    (((1,), (1,)), ((), ())),
                    preferred_element_type=jnp.float32,
                )
                inner_sum = inner_sum.reshape(fold_piece_rows, 2, RO)
                col_slice = col_one.astype(jnp.float32)
                added = jnp.sum(inner_sum * col_slice[:, None, :], axis=0)
                current = lax.dynamic_index_in_dim(partial_value, spoke_index, 0, keepdims=False)
                return lax.dynamic_update_index_in_dim(
                    partial_value, current + added, spoke_index, 0
                )

            sample_model = lax.fori_loop(
                0, my_share, fold_one_spoke, jnp.zeros((n_load, 2, RO), jnp.float32)
            )
            weighted = density[None, None, :] * (sample_model - target_data)
        grid_term = grid_rows(weighted)
        owned_rows = lax.psum_scatter(
            grid_term(jnp.int32(0), row_count * lax.axis_size(("tile", "spk"))),
            ("tile", "spk"),
            scatter_dimension=0,
            tiled=True,
        )
        partial_back = jnp.einsum("vpu,puqr->vqr", owned_rows, inv_table, precision=HIGH)
        returned = lax.all_to_all(
            partial_back, ("tile", "spk"), split_axis=2, concat_axis=0, tiled=True
        )
        coil_back = jnp.einsum("vpr,pvqc->rqc", returned, inv_table, precision=HIGH)
        gradient = lax.psum(conj_mul(coil_sens, coil_back), "coil")
        estimate = wavelet_shrink(estimate - STEP_SIZE * gradient, thresholds, LEVELS)
    return estimate


def solution(mesh):
    placed = (
        P("coil", ("grp", "tile", "spk"), None, None),
        P("coil", ("grp", "tile", "spk"), None, None),
        P(("grp", "tile", "spk"), None, None),
        P(("grp", "tile", "spk"), None),
        P(("grp", "tile", "spk")),
        P(),
    )
    return jax.shard_map(
        local,
        mesh=mesh,
        in_specs=placed,
        out_specs=P(("grp", "tile", "spk"), None, None),
        check_vma=False,
    )
```

profile of v0, /device:TPU:0, one launch (start us, length us, event | category | flops | bytes accessed | tf_op | source)
XLA Modules:
  0.0 512.3 jit_solution(6684872715194408570)
XLA Ops:
  9.2 10.6 %all-reduce = s32[8]{0:T(128)S(1)} all-reduce(s32[8]{0:T(128)S(1)} %dynamic-update-slice), channel_id=1, replica_groups=mesh['grp'=2,'tile'=4,'coil'=2,'spk'=2] {'tile','spk'}, use_global_device_ids=true, to_apply=%add | all-reduce | flops 8 | bytes 64
  22.5 3.3 all-to-all-start
  34.2 5.0 all-to-all-start.1
  39.9 5.1 all-to-all-done.1
  47.7 7.5 %while.98 = (s32[]{:T(128)}, f32[256,2,256]{2,0,1:T(8,128)}, bf16[4,256,256]{2,1,0:T(8,128)(2,1)S(1)}, f32[4,2,256]{2,1,0:T(2,128)S(1)}, bf16[4,256,256]{2,1,0:T(8,128)(2,1)S(1)}, /*index=5*/s32[]{:T(128)}, s32[]{:T(128)}) while((s32[]{:T(128)}, f32[256,2,256]{2,0,1:T(8,128)}, bf16[4,256,256]{2,1,0:T(8,128)(2,1)S(1)}, ...), condition=%wide.region_3.4_spmd.clone, body=%wide.region_2.3_spmd.clone.sunk | while | flops 67698688 | bytes 1841251 | solution.py:166
  48.8 2.1 convolution_add_fusion.8
  51.0 2.1 convolution_add_fusion.8
  53.1 2.1 convolution_add_fusion.8
  57.0 2.7 select_select_fusion
  60.5 24.4 %reduce-scatter.5.cloned.1.call-done = f32[32,2,256]{2,0,1:T(8,128)} async-done(((f32[256,2,256]{2,0,1:T(8,128)}), f32[32,2,256]{2,0,1:T(8,128)}) %reduce-scatter.5.cloned.1.call-update) | async-done | bytes 65552 | tf_op jit(solution)/shard_map/reduce_scatter | solution.py:211
  87.3 1.9 reshape.880
  89.2 3.4 all-to-all-start.2
  94.6 3.8 all-to-all-done.2
  102.2 1.8 copy.229
  107.4 18.6 %all-reduce.6.cloned.1.call-done = f32[32,2,256]{2,0,1:T(8,128)} async-done(((f32[32,2,256]{2,0,1:T(8,128)}), f32[32,2,256]{2,0,1:T(8,128)}) %all-reduce.6.cloned.1.call-update) | async-done | bytes 65552 | tf_op jit(solution)/shard_map/psum | solution.py:222
  129.7 1.7 copy.125
  131.3 1.9 reshape.882
  133.2 4.6 all-to-all-start.3
  138.6 5.2 %all-to-all-done.3 = f32[8,1,2048]{2,1,0:T(1,128)} async-done(((f32[8,1,2048]{2,1,0:T(1,128)}), f32[8,1,2048]{2,1,0:T(1,128)}, u32[]{:S(2)}, u32[]{:S(2)}) %all-to-all-start.3) | async-done | bytes 65568 | tf_op jit(solution)/shard_map/all_to_all | solution.py:179
  143.8 2.2 reduce.1
  146.1 1.8 reshape.883
  147.9 1.8 copy.228
  149.7 1.7 reshape.848
  152.9 14.2 %all_gather.13 = bf16[256,2,256]{2,0,1:T(8,128)(2,1)S(1)} all-gather(bf16[32,2,256]{2,0,1:T(8,128)(2,1)S(1)} %fusion.32), channel_id=1, replica_groups=mesh['grp'=2,'tile'=4,'coil'=2,'spk'=2] {'tile','spk'}, dimensions={0}, use_global_device_ids=true | all-gather | bytes 294912 | tf_op jit(solution)/shard_map/all_gather | solution.py:185
  168.1 12.7 %while.95 = (s32[]{:T(128)}, f32[4,2,256]{2,1,0:T(2,128)}, bf16[4,256,256]{2,1,0:T(8,128)(2,1)S(1)}, bf16[512,256]{1,0:T(8,128)(2,1)S(1)}, bf16[4,256,256]{2,1,0:T(8,128)(2,1)S(1)}, /*index=5*/s32[]{:T(128)}) while((s32[]{:T(128)}, f32[4,2,256]{2,1,0:T(2,128)}, bf16[4,256,256]{2,1,0:T(8,128)(2,1)S(1)}, bf16[512,256]{1,0:T(8,128)(2,1)S(1)}, ...), condition=%wide.region_8.9_spmd, body=%wide.region_6.8_spmd.sunk | while | flops 67436544 | bytes 6300293 | solution.py:206
  182.3 7.5 %while.99 = (s32[]{:T(128)}, f32[256,2,256]{2,0,1:T(8,128)}, bf16[4,256,256]{2,1,0:T(8,128)(2,1)S(1)}, f32[4,2,256]{2,1,0:T(2,128)S(1)}, bf16[4,256,256]{2,1,0:T(8,128)(2,1)S(1)}, /*index=5*/s32[]{:T(128)}, s32[]{:T(128)}) while((s32[]{:T(128)}, f32[256,2,256]{2,0,1:T(8,128)}, bf16[4,256,256]{2,1,0:T(8,128)(2,1)S(1)}, ...), condition=%wide.region_10.11_spmd.clone, body=%wide.region_9.10_spmd.clone.sunk | while | flops 67698688 | bytes 1841251 | solution.py:166
  183.4 2.1 convolution_add_fusion.9
  185.5 2.1 convolution_add_fusion.9
  187.6 2.1 convolution_add_fusion.9
  189.8 28.9 %reduce-scatter.7.cloned.1.call-done = f32[32,2,256]{2,0,1:T(8,128)} async-done(((f32[256,2,256]{2,0,1:T(8,128)}), f32[32,2,256]{2,0,1:T(8,128)}) %reduce-scatter.7.cloned.1.call-update) | async-done | bytes 65552 | tf_op jit(solution)/shard_map/reduce_scatter | solution.py:211
  220.7 8.3 %all_to_all.136 = f32[8,1,2048]{2,1,0:T(1,128)S(1)} all-to-all(f32[8,1,2048]{2,1,0:T(1,128)S(1)} %reshape.884), channel_id=1, replica_groups=mesh['grp'=2,'tile'=4,'coil'=2,'spk'=2] {'tile','spk'}, dimensions={0} | all-to-all | bytes 131072 | tf_op jit(solution)/shard_map/all_to_all | solution.py:218
  231.7 19.7 %all-reduce.8.cloned.1.call-done = f32[32,2,256]{2,0,1:T(8,128)} async-done(((f32[32,2,256]{2,0,1:T(8,128)}), f32[32,2,256]{2,0,1:T(8,128)}) %all-reduce.8.cloned.1.call-update) | async-done | bytes 65552 | tf_op jit(solution)/shard_map/psum | solution.py:222
  257.0 1.9 reshape.886
  258.9 4.6 all-to-all-start.5
  263.5 6.0 %all-to-all-done.5 = f32[8,1,2048]{2,1,0:T(1,128)} async-done(((f32[8,1,2048]{2,1,0:T(1,128)}), f32[8,1,2048]{2,1,0:T(1,128)}, u32[]{:S(2)}, u32[]{:S(2)}) %all-to-all-start.5) | async-done | bytes 65568 | tf_op jit(solution)/shard_map/all_to_all | solution.py:179
  269.5 2.2 reduce.3
  271.7 1.8 reshape.887
  273.5 1.8 copy.226
  275.3 1.7 reshape.857
  278.6 14.2 %all_gather.14 = bf16[256,2,256]{2,0,1:T(8,128)(2,1)S(1)} all-gather(bf16[32,2,256]{2,0,1:T(8,128)(2,1)S(1)} %fusion.33), channel_id=1, replica_groups=mesh['grp'=2,'tile'=4,'coil'=2,'spk'=2] {'tile','spk'}, dimensions={0}, use_global_device_ids=true | all-gather | bytes 294912 | tf_op jit(solution)/shard_map/all_gather | solution.py:185
  293.8 12.7 %while.96 = (s32[]{:T(128)}, f32[4,2,256]{2,1,0:T(2,128)}, bf16[4,256,256]{2,1,0:T(8,128)(2,1)S(1)}, bf16[512,256]{1,0:T(8,128)(2,1)S(1)}, bf16[4,256,256]{2,1,0:T(8,128)(2,1)S(1)}, /*index=5*/s32[]{:T(128)}) while((s32[]{:T(128)}, f32[4,2,256]{2,1,0:T(2,128)}, bf16[4,256,256]{2,1,0:T(8,128)(2,1)S(1)}, bf16[512,256]{1,0:T(8,128)(2,1)S(1)}, ...), condition=%wide.region_15.16_spmd, body=%wide.region_13.15_spmd.sunk | while | flops 67436544 | bytes 6300293 | solution.py:206
  307.9 7.5 %while.100 = (s32[]{:T(128)}, f32[256,2,256]{2,0,1:T(8,128)}, bf16[4,256,256]{2,1,0:T(8,128)(2,1)S(1)}, f32[4,2,256]{2,1,0:T(2,128)S(1)}, bf16[4,256,256]{2,1,0:T(8,128)(2,1)S(1)}, /*index=5*/s32[]{:T(128)}, s32[]{:T(128)}) while((s32[]{:T(128)}, f32[256,2,256]{2,0,1:T(8,128)}, bf16[4,256,256]{2,1,0:T(8,128)(2,1)S(1)}, ...), condition=%wide.region_17.18_spmd.clone, body=%wide.region_16.17_spmd.clone.sunk | while | flops 67698688 | bytes 1841251 | solution.py:166
  309.0 2.1 convolution_add_fusion.10
  311.1 2.1 convolution_add_fusion.10
  313.3 2.1 convolution_add_fusion.10
  315.6 28.8 %reduce-scatter.9.cloned.1.call-done = f32[32,2,256]{2,0,1:T(8,128)} async-done(((f32[256,2,256]{2,0,1:T(8,128)}), f32[32,2,256]{2,0,1:T(8,128)}) %reduce-scatter.9.cloned.1.call-update) | async-done | bytes 65552 | tf_op jit(solution)/shard_map/reduce_scatter | solution.py:211
  346.4 8.3 %all_to_all.137 = f32[8,1,2048]{2,1,0:T(1,128)S(1)} all-to-all(f32[8,1,2048]{2,1,0:T(1,128)S(1)} %reshape.888), channel_id=1, replica_groups=mesh['grp'=2,'tile'=4,'coil'=2,'spk'=2] {'tile','spk'}, dimensions={0} | all-to-all | bytes 131072 | tf_op jit(solution)/shard_map/all_to_all | solution.py:218
  357.4 19.5 %all-reduce.10.cloned.1.call-done = f32[32,2,256]{2,0,1:T(8,128)} async-done(((f32[32,2,256]{2,0,1:T(8,128)}), f32[32,2,256]{2,0,1:T(8,128)}) %all-reduce.10.cloned.1.call-update) | async-done | bytes 65552 | tf_op jit(solution)/shard_map/psum | solution.py:222
  382.5 1.9 reshape.890
  384.4 4.6 all-to-all-start.7
  389.0 6.0 %all-to-all-done.7 = f32[8,1,2048]{2,1,0:T(1,128)} async-done(((f32[8,1,2048]{2,1,0:T(1,128)}), f32[8,1,2048]{2,1,0:T(1,128)}, u32[]{:S(2)}, u32[]{:S(2)}) %all-to-all-start.7) | async-done | bytes 65568 | tf_op jit(solution)/shard_map/all_to_all | solution.py:179
  395.0 2.2 reduce.5
  397.2 1.8 reshape.891
  399.0 1.8 copy.224
  400.8 1.7 reshape.866
  404.1 14.2 %all_gather.15 = bf16[256,2,256]{2,0,1:T(8,128)(2,1)S(1)} all-gather(bf16[32,2,256]{2,0,1:T(8,128)(2,1)S(1)} %fusion.34), channel_id=1, replica_groups=mesh['grp'=2,'tile'=4,'coil'=2,'spk'=2] {'tile','spk'}, dimensions={0}, use_global_device_ids=true | all-gather | bytes 294912 | tf_op jit(solution)/shard_map/all_gather | solution.py:185
  419.3 12.7 %while.97 = (s32[]{:T(128)}, f32[4,2,256]{2,1,0:T(2,128)}, bf16[4,256,256]{2,1,0:T(8,128)(2,1)S(1)}, bf16[512,256]{1,0:T(8,128)(2,1)S(1)}, bf16[4,256,256]{2,1,0:T(8,128)(2,1)S(1)}, /*index=5*/s32[]{:T(128)}) while((s32[]{:T(128)}, f32[4,2,256]{2,1,0:T(2,128)}, bf16[4,256,256]{2,1,0:T(8,128)(2,1)S(1)}, bf16[512,256]{1,0:T(8,128)(2,1)S(1)}, ...), condition=%wide.region_22.23_spmd, body=%wide.region_20.22_spmd.sunk | while | flops 67436544 | bytes 6300293 | solution.py:206
  433.5 7.5 %while.101 = (s32[]{:T(128)}, f32[256,2,256]{2,0,1:T(8,128)}, bf16[4,256,256]{2,1,0:T(8,128)(2,1)S(1)}, f32[4,2,256]{2,1,0:T(2,128)S(1)}, bf16[4,256,256]{2,1,0:T(8,128)(2,1)S(1)}, /*index=5*/s32[]{:T(128)}, s32[]{:T(128)}) while((s32[]{:T(128)}, f32[256,2,256]{2,0,1:T(8,128)}, bf16[4,256,256]{2,1,0:T(8,128)(2,1)S(1)}, ...), condition=%wide.region_24.25_spmd.clone, body=%wide.region_23.24_spmd.clone.sunk | while | flops 67698688 | bytes 1841251 | solution.py:166
  434.6 2.1 convolution_add_fusion.11
  436.7 2.1 convolution_add_fusion.11
  438.9 2.1 convolution_add_fusion.11
  441.0 28.9 %reduce-scatter.11.cloned.1.call-done = f32[32,2,256]{2,0,1:T(8,128)} async-done(((f32[256,2,256]{2,0,1:T(8,128)}), f32[32,2,256]{2,0,1:T(8,128)}) %reduce-scatter.11.cloned.1.call-update) | async-done | bytes 65552 | tf_op jit(solution)/shard_map/reduce_scatter | solution.py:211
  472.0 8.3 %all_to_all.138 = f32[8,1,2048]{2,1,0:T(1,128)S(1)} all-to-all(f32[8,1,2048]{2,1,0:T(1,128)S(1)} %reshape.892), channel_id=1, replica_groups=mesh['grp'=2,'tile'=4,'coil'=2,'spk'=2] {'tile','spk'}, dimensions={0} | all-to-all | bytes 131072 | tf_op jit(solution)/shard_map/all_to_all | solution.py:218
  483.0 19.5 %all-reduce.12.cloned.1.call-done = f32[32,2,256]{2,0,1:T(8,128)} async-done(((f32[32,2,256]{2,0,1:T(8,128)}), f32[32,2,256]{2,0,1:T(8,128)}) %all-reduce.12.cloned.1.call-update) | async-done | bytes 65552 | tf_op jit(solution)/shard_map/psum | solution.py:222
  (390 shorter events, 117.0 us)
Async XLA Ops:
  6.5 14.8 %copy-start = (s32[8,256]{1,0:T(8,128)S(1)}, s32[8,256]{1,0:T(8,128)}, u32[]{:S(2)}) copy-start(s32[8,256]{1,0:T(8,128)} %param.23) | copy-start | bytes 24580
  22.5 11.7 %all-to-all-start = ((s32[8,1,256]{2,1,0:T(1,128)}), s32[8,1,256]{2,1,0:T(1,128)S(1)}, u32[]{:S(2)}, u32[]{:S(2)}) async-start(s32[8,1,256]{2,1,0:T(1,128)} %copy.115), calls=%async_computation | async-start | bytes 16384 | tf_op jit(solution)/shard_map/all_to_all | solution.py:132
  27.9 31.9 %copy-start.26 = (s32[8]{0:T(128)}, s32[8]{0:T(128)S(1)}, u32[]{:S(2)}) copy-start(s32[8]{0:T(128)S(1)} %get-tuple-element.881) | copy-start | bytes 100
  27.9 31.9 %copy-start.28 = (s32[8]{0:T(128)}, s32[8]{0:T(128)S(1)}, u32[]{:S(2)}) copy-start(s32[8]{0:T(128)S(1)} %get-tuple-element.882) | copy-start | bytes 100
  28.9 0.7 copy-start.19
  29.7 1.3 copy-start.23
  31.2 120.2 %copy-start.1 = (f32[1,256,2,256]{3,1,2,0:T(8,128)}, f32[1,256,2,256]{3,1,2,0:T(8,128)S(1)}, u32[]{:S(2)}) copy-start(f32[1,256,2,256]{3,1,2,0:T(8,128)S(1)} %get-tuple-element.830) | copy-start | bytes 1572868
  31.2 120.2 %copy-start.4 = (f32[1,256,2,256]{3,1,2,0:T(8,128)}, f32[1,256,2,256]{3,1,2,0:T(8,128)S(1)}, u32[]{:S(2)}) copy-start(f32[1,256,2,256]{3,1,2,0:T(8,128)S(1)} %get-tuple-element.833) | copy-start | bytes 1572868
  34.2 10.8 %all-to-all-start.1 = ((bf16[8,1,8,256]{3,2,1,0:T(8,128)(2,1)}), bf16[8,1,8,256]{3,2,1,0:T(8,128)(2,1)S(1)}, u32[]{:S(2)}, u32[]{:S(2)}) async-start(bf16[8,1,8,256]{3,2,1,0:T(8,128)(2,1)} %bitcast.26), calls=%async_computation.1 | async-start | bytes 65536 | tf_op jit(solution)/shard_map/all_to_all | solution.py:129
  39.2 45.7 %reduce-scatter.5.cloned.1.call-start = ((), (), s32[]{:S(2)}) async-start(), calls=%async_computation.13 | async-start | bytes 589824 | tf_op jit(solution)/shard_map/reduce_scatter | solution.py:211
  89.2 9.2 %all-to-all-start.2 = ((f32[8,1,2048]{2,1,0:T(1,128)}), f32[8,1,2048]{2,1,0:T(1,128)S(1)}, u32[]{:S(2)}, u32[]{:S(2)}) async-start(f32[8,1,2048]{2,1,0:T(1,128)} %reshape.880), calls=%async_computation.3 | async-start | bytes 131072 | tf_op jit(solution)/shard_map/all_to_all | solution.py:218
  92.6 33.5 %all-reduce.6.cloned.1.call-start = ((), (), s32[]{:S(2)}) async-start(), calls=%async_computation.14 | async-start | bytes 131072 | tf_op jit(solution)/shard_map/psum | solution.py:222
  105.8 0.7 copy-start.31
  106.5 0.7 copy-start.32
  106.5 0.7 copy-start.33
  106.5 0.7 copy-start.34
  106.5 0.7 copy-start.35
  106.5 0.7 copy-start.27
  106.5 0.7 copy-start.29
  106.5 0.7 copy-start.30
  127.0 0.7 copy-start.14
  133.2 10.6 %all-to-all-start.3 = ((f32[8,1,2048]{2,1,0:T(1,128)}), f32[8,1,2048]{2,1,0:T(1,128)}, u32[]{:S(2)}, u32[]{:S(2)}) async-start(f32[8,1,2048]{2,1,0:T(1,128)} %reshape.882), calls=%async_computation.4 | async-start | bytes 131072 | tf_op jit(solution)/shard_map/all_to_all | solution.py:179
  137.8 80.9 %reduce-scatter.7.cloned.1.call-start = ((), (), s32[]{:S(2)}) async-start(), calls=%async_computation.15 | async-start | bytes 589824 | tf_op jit(solution)/shard_map/reduce_scatter | solution.py:211
  168.1 0.7 copy-start.9
  169.7 1.6 copy-start.10
  171.3 0.7 copy-start.9
  172.8 1.6 copy-start.10
  174.5 0.7 copy-start.9
  176.0 1.6 copy-start.10
  177.7 0.7 copy-start.9
  179.2 1.6 copy-start.10
  180.8 0.7 copy-start.20
  189.7 61.7 %all-reduce.8.cloned.1.call-start = ((), (), s32[]{:S(2)}) async-start(), calls=%async_computation.16 | async-start | bytes 131072 | tf_op jit(solution)/shard_map/psum | solution.py:222
  251.5 1.4 copy-start.15
  252.5 1.0 copy-start.5
  252.9 1.1 copy-start.2
  258.9 10.6 %all-to-all-start.5 = ((f32[8,1,2048]{2,1,0:T(1,128)}), f32[8,1,2048]{2,1,0:T(1,128)}, u32[]{:S(2)}, u32[]{:S(2)}) async-start(f32[8,1,2048]{2,1,0:T(1,128)} %reshape.886), calls=%async_computation.7 | async-start | bytes 131072 | tf_op jit(solution)/shard_map/all_to_all | solution.py:179
  263.5 81.0 %reduce-scatter.9.cloned.1.call-start = ((), (), s32[]{:S(2)}) async-start(), calls=%async_computation.17 | async-start | bytes 589824 | tf_op jit(solution)/shard_map/reduce_scatter | solution.py:211
  293.8 0.7 copy-start.11
  295.3 1.6 copy-start.12
  296.9 0.7 copy-start.11
  298.5 1.6 copy-start.12
  300.1 0.7 copy-start.11
  301.6 1.6 copy-start.12
  303.3 0.7 copy-start.11
  304.8 1.6 copy-start.12
  306.5 0.7 copy-start.21
  315.4 61.6 %all-reduce.10.cloned.1.call-start = ((), (), s32[]{:S(2)}) async-start(), calls=%async_computation.18 | async-start | bytes 131072 | tf_op jit(solution)/shard_map/psum | solution.py:222
  377.0 1.4 copy-start.16
  378.0 1.0 copy-start.6
  378.4 1.1 copy-start.3
  384.4 10.6 %all-to-all-start.7 = ((f32[8,1,2048]{2,1,0:T(1,128)}), f32[8,1,2048]{2,1,0:T(1,128)}, u32[]{:S(2)}, u32[]{:S(2)}) async-start(f32[8,1,2048]{2,1,0:T(1,128)} %reshape.890), calls=%async_computation.10 | async-start | bytes 131072 | tf_op jit(solution)/shard_map/all_to_all | solution.py:179
  389.0 81.0 %reduce-scatter.11.cloned.1.call-start = ((), (), s32[]{:S(2)}) async-start(), calls=%async_computation.19 | async-start | bytes 589824 | tf_op jit(solution)/shard_map/reduce_scatter | solution.py:211
  419.3 0.7 copy-start.7
  420.9 1.6 copy-start.8
  422.5 0.7 copy-start.7
  424.0 1.6 copy-start.8
  425.7 0.7 copy-start.7
  427.2 1.6 copy-start.8
  428.9 0.7 copy-start.7
  430.4 1.6 copy-start.8
  432.1 0.7 copy-start.22
  441.0 61.5 %all-reduce.12.cloned.1.call-start = ((), (), s32[]{:S(2)}) async-start(), calls=%async_computation.20 | async-start | bytes 131072 | tf_op jit(solution)/shard_map/psum | solution.py:222
  503.6 0.7 copy-start.17
  (4 other events, 2.5 us)
Sparse Core Ops, SparseCore 0:
  55.3 29.5 reduce-scatter.4
  106.6 19.3 all-reduce.5
  189.9 28.8 reduce-scatter.6
  231.9 19.5 all-reduce.7
  315.5 28.9 reduce-scatter.8
  357.6 19.3 all-reduce.9
  441.1 28.8 reduce-scatter.10
  483.1 19.3 all-reduce.11
where the time goes:
time: 516 us; the launch traced here: 512 us
  waiting for transfers between devices  215 us (42%)
  blocking collectives  78.2 us (15%)
  local copies, waits for them, and re-layouts  69.4 us (13%)
  matrix products  62 us (12%)
  other arithmetic  46.1 us (9%)
  starting transfers between devices  26.2 us (5%)
  between operations  15.1 us (3%)
    reduce_scatter x4, waiting for transfers between devices, local(): lax.psum_scatter(grid_term(jnp.int32(0), row_count * lax.axis_size(('tile...  111 us
    psum x4, waiting for transfers between devices, local(): gradient = lax.psum(conj_mul(coil_sens, coil_back), 'coil')  77.4 us
    all_gather x3, blocking collectives, local(): piece = lax.all_gather(kspace, ('tile', 'spk'), axis=0, tiled=True)  42.6 us
    dot_general x16, matrix products, grid_one_spoke(): jnp.dot(smeared.reshape(piece_rows * 2, RO), row_one, preferred_element_t...  29.2 us
    all_to_all x3, blocking collectives, local(): lax.all_to_all(partial_back, ('tile', 'spk'), split_axis=2, concat_axis=0...  24.9 us
    unnamed x82, local copies, waits for them, and re-layouts  24.4 us
    all_to_all x3, waiting for transfers between devices, local(): lax.all_to_all(half_done, ('tile', 'spk'), split_axis=2, concat_axis=0, t...  17.1 us
    dynamic_update_slice x12, other arithmetic, fold_one_spoke(): lax.dynamic_update_index_in_dim(partial_value, current + added, spoke_ind...  15.1 us
  transfers between devices with their start and end apart: 14, of which 13 were waited for; matrix products, arithmetic and copies ran while one was open for 3% of the time, Pallas kernels for 0%

commit v1 on v0

--- a/solution.py
+++ b/solution.py
@@ -219,7 +219,7 @@
             partial_back, ("tile", "spk"), split_axis=2, concat_axis=0, tiled=True
         )
         coil_back = jnp.einsum("vpr,pvqc->rqc", returned, inv_table, precision=HIGH)
-        gradient = lax.psum(conj_mul(coil_sens, coil_back), "coil")
+        gradient = jnp.sum(lax.all_gather(conj_mul(coil_sens, coil_back), "coil"), axis=0)
         estimate = wavelet_shrink(estimate - STEP_SIZE * gradient, thresholds, LEVELS)
     return estimate
 

time: 516 us -> 463 us (0.90)
  waiting for transfers between devices: 215 us -> 139 us
  blocking collectives: 78.2 us -> 98.3 us
  matrix products: 62 us -> 70.9 us
    psum x4 -> x0, waiting for transfers between devices: 77.4 us -> none  [local(): gradient = lax.psum(conj_mul(coil_sens, coil_back), 'coil')]
    all_gather x0 -> x4, blocking collectives: none -> 19.8 us  [local(): lax.all_gather(conj_mul(coil_sens, coil_back), 'coil')]
    dot_general x12, matrix products: 3.06 us -> 14.5 us  [fold_one_spoke(): lax.dot_general(flat_piece, row_one, (((1,), (1,)), ((), ())), preferred_...]
    while x48 -> x0, local copies, waits for them, and re-layouts: 8.62 us -> none
    unnamed x82 -> x88, local copies, waits for them, and re-layouts: 24.4 us -> 25.8 us
  transfers between devices with their start and end apart: 14 -> 10, of which waited for: 13 -> 9; matrix products, arithmetic and copies ran while one was open for 3% -> 4% of each run, Pallas kernels for 0% -> 0%
where the time goes in v1:
time: 463 us; the launch traced here: 459 us
  waiting for transfers between devices  139 us (30%)
  blocking collectives  98.3 us (21%)
  matrix products  70.9 us (15%)
  local copies, waits for them, and re-layouts  64.3 us (14%)
  other arithmetic  47.4 us (10%)
  starting transfers between devices  23.9 us (5%)
  between operations  14.7 us (3%)
    reduce_scatter x4, waiting for transfers between devices, local(): lax.psum_scatter(grid_term(jnp.int32(0), row_count * lax.axis_size(('tile...  112 us
    all_gather x3, blocking collectives, local(): piece = lax.all_gather(kspace, ('tile', 'spk'), axis=0, tiled=True)  42.9 us
    dot_general x16, matrix products, grid_one_spoke(): jnp.dot(smeared.reshape(piece_rows * 2, RO), row_one, preferred_element_t...  29.3 us
    unnamed x88, local copies, waits for them, and re-layouts  25.8 us
    all_to_all x3, blocking collectives, local(): lax.all_to_all(partial_back, ('tile', 'spk'), split_axis=2, concat_axis=0...  24.9 us
    all_gather x4, blocking collectives, local(): lax.all_gather(conj_mul(coil_sens, coil_back), 'coil')  19.8 us
    all_to_all x3, waiting for transfers between devices, local(): lax.all_to_all(half_done, ('tile', 'spk'), split_axis=2, concat_axis=0, t...  16.8 us
    dynamic_update_slice x12, other arithmetic, fold_one_spoke(): lax.dynamic_update_index_in_dim(partial_value, current + added, spoke_ind...  15.1 us
  transfers between devices with their start and end apart: 10, of which 9 were waited for; matrix products, arithmetic and copies ran while one was open for 4% of the time, Pallas kernels for 0%

profile of v1, /device:TPU:0, one launch (start us, length us, event | category | flops | bytes accessed | tf_op | source)
XLA Modules:
  0.0 458.7 jit_solution(15881640661366813184)
XLA Ops:
  9.2 10.6 %all-reduce = s32[8]{0:T(128)S(1)} all-reduce(s32[8]{0:T(128)S(1)} %dynamic-update-slice), channel_id=1, replica_groups=mesh['grp'=2,'tile'=4,'coil'=2,'spk'=2] {'tile','spk'}, use_global_device_ids=true, to_apply=%add | all-reduce | flops 8 | bytes 64
  22.5 3.3 all-to-all-start
  38.0 5.0 %all-to-all-start.1 = ((bf16[8,1,8,256]{3,2,1,0:T(8,128)(2,1)}), bf16[8,1,8,256]{3,2,1,0:T(8,128)(2,1)S(1)}, u32[]{:S(2)}, u32[]{:S(2)}) async-start(bf16[8,1,8,256]{3,2,1,0:T(8,128)(2,1)} %bitcast.26), calls=%async_computation.1 | async-start | bytes 65536 | tf_op jit(solution)/shard_map/all_to_all | solution.py:129
  43.7 5.1 %all-to-all-done.1 = bf16[8,1,8,256]{3,2,1,0:T(8,128)(2,1)S(1)} async-done(((bf16[8,1,8,256]{3,2,1,0:T(8,128)(2,1)}), bf16[8,1,8,256]{3,2,1,0:T(8,128)(2,1)S(1)}, u32[]{:S(2)}, u32[]{:S(2)}) %all-to-all-start.1) | async-done | bytes 32800 | tf_op jit(solution)/shard_map/all_to_all | solution.py:129
  51.5 7.5 %while.98 = (s32[]{:T(128)}, f32[256,2,256]{2,0,1:T(8,128)}, bf16[4,256,256]{2,1,0:T(8,128)(2,1)S(1)}, f32[4,2,256]{2,1,0:T(2,128)S(1)}, bf16[4,256,256]{2,1,0:T(8,128)(2,1)S(1)}, /*index=5*/s32[]{:T(128)}, s32[]{:T(128)}) while((s32[]{:T(128)}, f32[256,2,256]{2,0,1:T(8,128)}, bf16[4,256,256]{2,1,0:T(8,128)(2,1)S(1)}, ...), condition=%wide.region_3.4_spmd.clone, body=%wide.region_2.3_spmd.clone.sunk | while | flops 67698688 | bytes 1841251 | solution.py:166
  52.7 2.1 convolution_add_fusion.8
  54.8 2.1 convolution_add_fusion.8
  57.0 2.1 convolution_add_fusion.8
  62.2 2.6 select_select_fusion
  66.3 22.6 %reduce-scatter.5.cloned.1.call-done = f32[32,2,256]{2,0,1:T(8,128)} async-done(((f32[256,2,256]{2,0,1:T(8,128)}), f32[32,2,256]{2,0,1:T(8,128)}) %reduce-scatter.5.cloned.1.call-update) | async-done | bytes 65552 | tf_op jit(solution)/shard_map/reduce_scatter | solution.py:211
  91.3 1.9 reshape.886
  93.1 3.4 all-to-all-start.2
  98.1 4.3 all-to-all-done.2
  106.1 1.8 copy.220
  109.8 5.0 %all-gather = f32[64,2,256]{2,0,1:T(8,128)} all-gather(f32[32,2,256]{2,0,1:T(8,128)S(1)} %pad_maximum_fusion.12), channel_id=2, replica_groups=mesh['grp'=2,'tile'=4,'coil'=2,'spk'=2] {'coil'}, dimensions={0}, use_global_device_ids=true | all-gather | bytes 196608 | tf_op jit(solution)/shard_map/all_gather | solution.py:222
  120.2 1.9 reshape.888
  122.1 4.0 all-to-all-start.3
  126.9 5.1 %all-to-all-done.3 = f32[8,1,2048]{2,1,0:T(1,128)} async-done(((f32[8,1,2048]{2,1,0:T(1,128)}), f32[8,1,2048]{2,1,0:T(1,128)}, u32[]{:S(2)}, u32[]{:S(2)}) %all-to-all-start.3) | async-done | bytes 65568 | tf_op jit(solution)/shard_map/all_to_all | solution.py:179
  132.0 2.3 reduce.1
  134.3 1.8 reshape.889
  136.1 1.8 copy.219
  137.9 1.7 reshape.854
  141.2 14.2 %all_gather.39 = bf16[256,2,256]{2,0,1:T(8,128)(2,1)S(1)} all-gather(bf16[32,2,256]{2,0,1:T(8,128)(2,1)S(1)} %fusion.32), channel_id=1, replica_groups=mesh['grp'=2,'tile'=4,'coil'=2,'spk'=2] {'tile','spk'}, dimensions={0}, use_global_device_ids=true | all-gather | bytes 294912 | tf_op jit(solution)/shard_map/all_gather | solution.py:185
  157.1 13.6 %while.95 = (s32[]{:T(128)}, f32[4,2,256]{2,1,0:T(2,128)}, bf16[4,256,256]{2,1,0:T(8,128)(2,1)S(1)}, bf16[512,256]{1,0:T(8,128)(2,1)}, bf16[4,256,256]{2,1,0:T(8,128)(2,1)S(1)}, /*index=5*/s32[]{:T(128)}) while((s32[]{:T(128)}, f32[4,2,256]{2,1,0:T(2,128)}, bf16[4,256,256]{2,1,0:T(8,128)(2,1)S(1)}, bf16[512,256]{1,0:T(8,128)(2,1)}, ...), condition=%wide.region_8.9_spmd, body=%wide.region_6.8_spmd.sunk | while | flops 67436544 | bytes 4203085 | solution.py:206
  172.1 7.5 %while.99 = (s32[]{:T(128)}, f32[256,2,256]{2,0,1:T(8,128)}, bf16[4,256,256]{2,1,0:T(8,128)(2,1)S(1)}, f32[4,2,256]{2,1,0:T(2,128)S(1)}, bf16[4,256,256]{2,1,0:T(8,128)(2,1)S(1)}, /*index=5*/s32[]{:T(128)}, s32[]{:T(128)}) while((s32[]{:T(128)}, f32[256,2,256]{2,0,1:T(8,128)}, bf16[4,256,256]{2,1,0:T(8,128)(2,1)S(1)}, ...), condition=%wide.region_10.11_spmd.clone, body=%wide.region_9.10_spmd.clone.sunk | while | flops 67698688 | bytes 1841251 | solution.py:166
  173.3 2.1 convolution_add_fusion.9
  175.4 2.1 convolution_add_fusion.9
  177.5 2.1 convolution_add_fusion.9
  179.7 29.8 %reduce-scatter.7.cloned.1.call-done = f32[32,2,256]{2,0,1:T(8,128)} async-done(((f32[256,2,256]{2,0,1:T(8,128)}), f32[32,2,256]{2,0,1:T(8,128)}) %reduce-scatter.7.cloned.1.call-update) | async-done | bytes 65552 | tf_op jit(solution)/shard_map/reduce_scatter | solution.py:211
  211.5 8.3 %all_to_all.136 = f32[8,1,2048]{2,1,0:T(1,128)S(1)} all-to-all(f32[8,1,2048]{2,1,0:T(1,128)S(1)} %reshape.890), channel_id=1, replica_groups=mesh['grp'=2,'tile'=4,'coil'=2,'spk'=2] {'tile','spk'}, dimensions={0} | all-to-all | bytes 131072 | tf_op jit(solution)/shard_map/all_to_all | solution.py:218
  221.9 4.9 %all-gather.1 = f32[64,2,256]{2,0,1:T(8,128)S(1)} all-gather(f32[32,2,256]{2,0,1:T(8,128)S(1)} %pad_maximum_fusion.13), channel_id=3, replica_groups=mesh['grp'=2,'tile'=4,'coil'=2,'spk'=2] {'coil'}, dimensions={0}, use_global_device_ids=true | all-gather | bytes 196608 | tf_op jit(solution)/shard_map/all_gather | solution.py:222
  230.0 1.7 copy.138
  231.6 1.9 reshape.892
  233.5 4.0 all-to-all-start.5
  237.5 5.9 %all-to-all-done.5 = f32[8,1,2048]{2,1,0:T(1,128)} async-done(((f32[8,1,2048]{2,1,0:T(1,128)}), f32[8,1,2048]{2,1,0:T(1,128)}, u32[]{:S(2)}, u32[]{:S(2)}) %all-to-all-start.5) | async-done | bytes 65568 | tf_op jit(solution)/shard_map/all_to_all | solution.py:179
  243.4 2.3 reduce.3
  245.7 1.8 reshape.893
  247.5 1.8 copy.217
  249.3 1.7 reshape.863
  252.6 14.4 %all_gather.42 = bf16[256,2,256]{2,0,1:T(8,128)(2,1)S(1)} all-gather(bf16[32,2,256]{2,0,1:T(8,128)(2,1)S(1)} %fusion.33), channel_id=1, replica_groups=mesh['grp'=2,'tile'=4,'coil'=2,'spk'=2] {'tile','spk'}, dimensions={0}, use_global_device_ids=true | all-gather | bytes 294912 | tf_op jit(solution)/shard_map/all_gather | solution.py:185
  268.7 13.6 %while.96 = (s32[]{:T(128)}, f32[4,2,256]{2,1,0:T(2,128)}, bf16[4,256,256]{2,1,0:T(8,128)(2,1)S(1)}, bf16[512,256]{1,0:T(8,128)(2,1)}, bf16[4,256,256]{2,1,0:T(8,128)(2,1)S(1)}, /*index=5*/s32[]{:T(128)}) while((s32[]{:T(128)}, f32[4,2,256]{2,1,0:T(2,128)}, bf16[4,256,256]{2,1,0:T(8,128)(2,1)S(1)}, bf16[512,256]{1,0:T(8,128)(2,1)}, ...), condition=%wide.region_15.16_spmd, body=%wide.region_13.15_spmd.sunk | while | flops 67436544 | bytes 4203085 | solution.py:206
  283.7 7.5 %while.100 = (s32[]{:T(128)}, f32[256,2,256]{2,0,1:T(8,128)}, bf16[4,256,256]{2,1,0:T(8,128)(2,1)S(1)}, f32[4,2,256]{2,1,0:T(2,128)S(1)}, bf16[4,256,256]{2,1,0:T(8,128)(2,1)S(1)}, /*index=5*/s32[]{:T(128)}, s32[]{:T(128)}) while((s32[]{:T(128)}, f32[256,2,256]{2,0,1:T(8,128)}, bf16[4,256,256]{2,1,0:T(8,128)(2,1)S(1)}, ...), condition=%wide.region_17.18_spmd.clone, body=%wide.region_16.17_spmd.clone.sunk | while | flops 67698688 | bytes 1841251 | solution.py:166
  284.9 2.1 convolution_add_fusion.10
  287.0 2.1 convolution_add_fusion.10
  289.2 2.1 convolution_add_fusion.10
  291.3 29.9 %reduce-scatter.9.cloned.1.call-done = f32[32,2,256]{2,0,1:T(8,128)} async-done(((f32[256,2,256]{2,0,1:T(8,128)}), f32[32,2,256]{2,0,1:T(8,128)}) %reduce-scatter.9.cloned.1.call-update) | async-done | bytes 65552 | tf_op jit(solution)/shard_map/reduce_scatter | solution.py:211
  323.1 8.3 %all_to_all.137 = f32[8,1,2048]{2,1,0:T(1,128)S(1)} all-to-all(f32[8,1,2048]{2,1,0:T(1,128)S(1)} %reshape.894), channel_id=1, replica_groups=mesh['grp'=2,'tile'=4,'coil'=2,'spk'=2] {'tile','spk'}, dimensions={0} | all-to-all | bytes 131072 | tf_op jit(solution)/shard_map/all_to_all | solution.py:218
  333.6 4.9 %all-gather.2 = f32[64,2,256]{2,0,1:T(8,128)S(1)} all-gather(f32[32,2,256]{2,0,1:T(8,128)S(1)} %pad_maximum_fusion.14), channel_id=4, replica_groups=mesh['grp'=2,'tile'=4,'coil'=2,'spk'=2] {'coil'}, dimensions={0}, use_global_device_ids=true | all-gather | bytes 196608 | tf_op jit(solution)/shard_map/all_gather | solution.py:222
  343.3 1.9 reshape.896
  345.2 4.0 all-to-all-start.7
  349.2 5.9 %all-to-all-done.7 = f32[8,1,2048]{2,1,0:T(1,128)} async-done(((f32[8,1,2048]{2,1,0:T(1,128)}), f32[8,1,2048]{2,1,0:T(1,128)}, u32[]{:S(2)}, u32[]{:S(2)}) %all-to-all-start.7) | async-done | bytes 65568 | tf_op jit(solution)/shard_map/all_to_all | solution.py:179
  355.1 2.3 reduce.5
  357.4 1.8 reshape.897
  359.1 1.8 copy.215
  361.0 1.7 reshape.872
  364.2 14.2 %all_gather.45 = bf16[256,2,256]{2,0,1:T(8,128)(2,1)S(1)} all-gather(bf16[32,2,256]{2,0,1:T(8,128)(2,1)S(1)} %fusion.34), channel_id=1, replica_groups=mesh['grp'=2,'tile'=4,'coil'=2,'spk'=2] {'tile','spk'}, dimensions={0}, use_global_device_ids=true | all-gather | bytes 294912 | tf_op jit(solution)/shard_map/all_gather | solution.py:185
  380.1 13.6 %while.97 = (s32[]{:T(128)}, f32[4,2,256]{2,1,0:T(2,128)}, bf16[4,256,256]{2,1,0:T(8,128)(2,1)S(1)}, bf16[512,256]{1,0:T(8,128)(2,1)}, bf16[4,256,256]{2,1,0:T(8,128)(2,1)S(1)}, /*index=5*/s32[]{:T(128)}) while((s32[]{:T(128)}, f32[4,2,256]{2,1,0:T(2,128)}, bf16[4,256,256]{2,1,0:T(8,128)(2,1)S(1)}, bf16[512,256]{1,0:T(8,128)(2,1)}, ...), condition=%wide.region_22.23_spmd, body=%wide.region_20.22_spmd.sunk | while | flops 67436544 | bytes 4203085 | solution.py:206
  395.2 7.5 %while.101 = (s32[]{:T(128)}, f32[256,2,256]{2,0,1:T(8,128)}, bf16[4,256,256]{2,1,0:T(8,128)(2,1)S(1)}, f32[4,2,256]{2,1,0:T(2,128)S(1)}, bf16[4,256,256]{2,1,0:T(8,128)(2,1)S(1)}, /*index=5*/s32[]{:T(128)}, s32[]{:T(128)}) while((s32[]{:T(128)}, f32[256,2,256]{2,0,1:T(8,128)}, bf16[4,256,256]{2,1,0:T(8,128)(2,1)S(1)}, ...), condition=%wide.region_24.25_spmd.clone, body=%wide.region_23.24_spmd.clone.sunk | while | flops 67698688 | bytes 1841251 | solution.py:166
  396.3 2.1 convolution_add_fusion.11
  398.5 2.1 convolution_add_fusion.11
  400.6 2.1 convolution_add_fusion.11
  402.7 30.0 %reduce-scatter.11.cloned.1.call-done = f32[32,2,256]{2,0,1:T(8,128)} async-done(((f32[256,2,256]{2,0,1:T(8,128)}), f32[32,2,256]{2,0,1:T(8,128)}) %reduce-scatter.11.cloned.1.call-update) | async-done | bytes 65552 | tf_op jit(solution)/shard_map/reduce_scatter | solution.py:211
  434.7 8.3 %all_to_all.138 = f32[8,1,2048]{2,1,0:T(1,128)S(1)} all-to-all(f32[8,1,2048]{2,1,0:T(1,128)S(1)} %reshape.898), channel_id=1, replica_groups=mesh['grp'=2,'tile'=4,'coil'=2,'spk'=2] {'tile','spk'}, dimensions={0} | all-to-all | bytes 131072 | tf_op jit(solution)/shard_map/all_to_all | solution.py:218
  445.1 4.9 %all-gather.3 = f32[64,2,256]{2,0,1:T(8,128)S(1)} all-gather(f32[32,2,256]{2,0,1:T(8,128)S(1)} %pad_maximum_fusion.15), channel_id=5, replica_groups=mesh['grp'=2,'tile'=4,'coil'=2,'spk'=2] {'coil'}, dimensions={0}, use_global_device_ids=true | all-gather | bytes 196608 | tf_op jit(solution)/shard_map/all_gather | solution.py:222
  (344 shorter events, 121.5 us)
Async XLA Ops:
  6.5 14.8 %copy-start = (s32[8,256]{1,0:T(8,128)S(1)}, s32[8,256]{1,0:T(8,128)}, u32[]{:S(2)}) copy-start(s32[8,256]{1,0:T(8,128)} %param.23) | copy-start | bytes 24580
  7.2 0.7 copy-start.20
  22.5 15.5 %all-to-all-start = ((s32[8,1,256]{2,1,0:T(1,128)}), s32[8,1,256]{2,1,0:T(1,128)S(1)}, u32[]{:S(2)}, u32[]{:S(2)}) async-start(s32[8,1,256]{2,1,0:T(1,128)} %copy.118), calls=%async_computation | async-start | bytes 16384 | tf_op jit(solution)/shard_map/all_to_all | solution.py:132
  27.8 37.0 %copy-start.21 = (s32[8]{0:T(128)}, s32[8]{0:T(128)S(1)}, u32[]{:S(2)}) copy-start(s32[8]{0:T(128)S(1)} %get-tuple-element.881) | copy-start | bytes 100
  27.8 37.0 %copy-start.23 = (s32[8]{0:T(128)}, s32[8]{0:T(128)S(1)}, u32[]{:S(2)}) copy-start(s32[8]{0:T(128)S(1)} %get-tuple-element.882) | copy-start | bytes 100
  32.7 0.7 copy-start.14
  33.4 0.7 copy-start.19
  33.4 1.3 copy-start.18
  34.9 104.7 %copy-start.1 = (f32[1,256,2,256]{3,1,2,0:T(8,128)}, f32[1,256,2,256]{3,1,2,0:T(8,128)S(1)}, u32[]{:S(2)}) copy-start(f32[1,256,2,256]{3,1,2,0:T(8,128)S(1)} %get-tuple-element.829) | copy-start | bytes 1572868
  35.0 104.7 %copy-start.4 = (f32[1,256,2,256]{3,1,2,0:T(8,128)}, f32[1,256,2,256]{3,1,2,0:T(8,128)S(1)}, u32[]{:S(2)}) copy-start(f32[1,256,2,256]{3,1,2,0:T(8,128)S(1)} %get-tuple-element.834) | copy-start | bytes 1572868
  36.8 1.2 copy-start.13
  38.0 10.8 %all-to-all-start.1 = ((bf16[8,1,8,256]{3,2,1,0:T(8,128)(2,1)}), bf16[8,1,8,256]{3,2,1,0:T(8,128)(2,1)S(1)}, u32[]{:S(2)}, u32[]{:S(2)}) async-start(bf16[8,1,8,256]{3,2,1,0:T(8,128)(2,1)} %bitcast.26), calls=%async_computation.1 | async-start | bytes 65536 | tf_op jit(solution)/shard_map/all_to_all | solution.py:129
  43.0 45.9 %reduce-scatter.5.cloned.1.call-start = ((), (), s32[]{:S(2)}) async-start(), calls=%async_computation.13 | async-start | bytes 589824 | tf_op jit(solution)/shard_map/reduce_scatter | solution.py:211
  49.3 0.6 copy-start.12
  59.1 0.7 copy-start.28
  59.1 0.7 copy-start.31
  61.4 0.6 copy-start.26
  61.4 0.6 copy-start.27
  61.4 0.6 copy-start.30
  64.8 0.7 copy-start.29
  93.1 9.2 %all-to-all-start.2 = ((f32[8,1,2048]{2,1,0:T(1,128)}), f32[8,1,2048]{2,1,0:T(1,128)S(1)}, u32[]{:S(2)}, u32[]{:S(2)}) async-start(f32[8,1,2048]{2,1,0:T(1,128)} %reshape.886), calls=%async_computation.3 | async-start | bytes 131072 | tf_op jit(solution)/shard_map/all_to_all | solution.py:218
  96.5 0.7 copy-start.32
  96.5 0.7 copy-start.22
  96.5 0.7 copy-start.24
  96.5 0.7 copy-start.25
  102.3 0.6 copy-start.7
  115.9 0.7 copy-start.8
  122.1 9.9 %all-to-all-start.3 = ((f32[8,1,2048]{2,1,0:T(1,128)}), f32[8,1,2048]{2,1,0:T(1,128)}, u32[]{:S(2)}, u32[]{:S(2)}) async-start(f32[8,1,2048]{2,1,0:T(1,128)} %reshape.888), calls=%async_computation.4 | async-start | bytes 131072 | tf_op jit(solution)/shard_map/all_to_all | solution.py:179
  126.1 83.4 %reduce-scatter.7.cloned.1.call-start = ((), (), s32[]{:S(2)}) async-start(), calls=%async_computation.14 | async-start | bytes 589824 | tf_op jit(solution)/shard_map/reduce_scatter | solution.py:211
  170.7 0.7 copy-start.15
  226.8 0.7 copy-start.9
  227.1 1.1 copy-start.5
  227.5 1.1 copy-start.2
  233.5 9.9 %all-to-all-start.5 = ((f32[8,1,2048]{2,1,0:T(1,128)}), f32[8,1,2048]{2,1,0:T(1,128)}, u32[]{:S(2)}, u32[]{:S(2)}) async-start(f32[8,1,2048]{2,1,0:T(1,128)} %reshape.892), calls=%async_computation.7 | async-start | bytes 131072 | tf_op jit(solution)/shard_map/all_to_all | solution.py:179
  237.5 83.7 %reduce-scatter.9.cloned.1.call-start = ((), (), s32[]{:S(2)}) async-start(), calls=%async_computation.15 | async-start | bytes 589824 | tf_op jit(solution)/shard_map/reduce_scatter | solution.py:211
  282.3 0.7 copy-start.16
  338.5 0.7 copy-start.10
  338.7 1.1 copy-start.6
  339.2 1.1 copy-start.3
  345.2 9.9 %all-to-all-start.7 = ((f32[8,1,2048]{2,1,0:T(1,128)}), f32[8,1,2048]{2,1,0:T(1,128)}, u32[]{:S(2)}, u32[]{:S(2)}) async-start(f32[8,1,2048]{2,1,0:T(1,128)} %reshape.896), calls=%async_computation.10 | async-start | bytes 131072 | tf_op jit(solution)/shard_map/all_to_all | solution.py:179
  349.1 83.6 %reduce-scatter.11.cloned.1.call-start = ((), (), s32[]{:S(2)}) async-start(), calls=%async_computation.16 | async-start | bytes 589824 | tf_op jit(solution)/shard_map/reduce_scatter | solution.py:211
  393.8 0.7 copy-start.17
  450.2 0.7 copy-start.11
Sparse Core Ops, SparseCore 0:
  59.2 29.6 reduce-scatter.4
  179.8 29.6 reduce-scatter.6
  291.4 29.7 reduce-scatter.8
  402.8 29.8 reduce-scatter.10
